TPU v7x, 128 devices: a whole 4x4x4 slice. The times are simulated.
128 devices in a mesh: tm: 64 (over z, y, x), state: 2 (over core).
Axes of the slice: x: 4, y: 4, z: 4, core: 2. Of those that a mesh axis runs over, the one named last changes fastest.
Arguments:
- symbols: int32 [8], P('state'), may hold values from 0 to 255
- emission: float32 [8192, 256], P('tm'), may hold values from 0.2 to 5
- decay: float32 [2, 8192], P('state', 'tm'), may hold values from 0.05 to 1
- left_factor: float32 [2, 64, 8192], P('state', None, 'tm'), may hold values from 0.1 to 3
- right_factor: float32 [2, 64, 8192], P('state', None, 'tm'), may hold values from 0.001 to 0.03
- initial: float32 [8192], P('tm'), may hold values from 0.1 to 10
Outputs:
- filtered: float32 [8, 8192], P('state', 'tm')
- log_scale: float32 [8], P('state')
All inputs are finite; a program needn't handle non-finite values.
Results may differ from a plain program's by a relative error of at most 0.00011.
Values sent between devices are 32-bit elements; how exact they have to be, the bound alone decides.
A program may use at most 64 MiB of HBM per device.

v0:
```python
import jax
import jax.numpy as jnp
from jax import lax
from jax.sharding import PartitionSpec as P

S = 8192


PRECISE = lax.Precision.HIGHEST


def copy_for_each(array, axis):
    copies = jnp.broadcast_to(array, (lax.axis_size(axis), *array.shape))
    return lax.all_to_all(copies, axis, split_axis=0, concat_axis=0, tiled=True)


def over_copies(array, axis):
    return copy_for_each(array, axis).sum(axis=0)


def in_one(arrays, axis):
    ends = [0]
    for a in arrays:
        ends.append(ends[-1] + a.size)
    running = over_copies(jnp.concatenate([a.ravel() for a in arrays]), axis)
    return tuple((running[b:e].reshape(a.shape) for a, b, e in zip(arrays, ends, ends[1:])))


def passed_along(value, axis, steps):
    count = lax.axis_size(axis)
    first, last = (max(0, -steps), min(count, count - steps))
    return lax.ppermute(value, axis, [(source, source + steps) for source in range(first, last)])


def run_span(entry_vec, emitted_all, decay_row, left_rows, right_rows):
    projected, total_sum = in_one(
        (jnp.dot(left_rows, entry_vec, precision=PRECISE), jnp.sum(entry_vec)), "tm"
    )
    rescale = S / total_sum
    belief = entry_vec * rescale
    mixture = projected * rescale / S

    def frame(state_pair, emitted):
        belief_now, mixture_now = state_pair
        unscaled = emitted * (
            decay_row * belief_now + jnp.dot(mixture_now, right_rows, precision=PRECISE)
        )
        proj_next, total_next = in_one(
            (jnp.dot(left_rows, unscaled, precision=PRECISE), jnp.sum(unscaled)), "tm"
        )
        normal = total_next / S
        belief_next = unscaled / normal
        mixture_next = proj_next / normal / S
        return ((belief_next, mixture_next), (belief_next, jnp.log(normal)))

    (closing, mixture_end), (beliefs, log_levels) = lax.scan(frame, (belief, mixture), emitted_all)
    return (beliefs, log_levels, closing)


def per_device(symbols, emission, decay, left_factor, right_factor, initial):
    decay_row = decay[0]
    left_rows = left_factor[0]
    right_rows = right_factor[0]
    onehot = (symbols[:, None] == jnp.arange(emission.shape[1], dtype=jnp.int32)[None, :]).astype(
        jnp.float32
    )
    emitted_all = jnp.einsum("fv,sv->fs", onehot, emission, precision=PRECISE)
    leader = lax.axis_index("state") == 0

    def pass_on(closing):
        return jnp.where(leader, initial, passed_along(closing, "state", 1))

    def section(step_idx, entry_vec):
        beliefs, log_levels, closing = run_span(
            entry_vec, emitted_all, decay_row, left_rows, right_rows
        )
        return pass_on(closing)

    entry_vec = lax.fori_loop(0, lax.axis_size("state") - 1, section, initial)
    beliefs, log_levels, closing = run_span(
        entry_vec, emitted_all, decay_row, left_rows, right_rows
    )
    return (beliefs, log_levels)


def solution(mesh):
    return jax.shard_map(
        per_device,
        mesh=mesh,
        in_specs=(
            P("state"),
            P("tm", None),
            P("state", "tm"),
            P("state", None, "tm"),
            P("state", None, "tm"),
            P("tm"),
        ),
        out_specs=(P("state", "tm"), P("state")),
        check_vma=False,
    )
```

profile of v0, /device:TPU:0, one launch (start us, length us, event | category | flops | bytes accessed | tf_op | source)
XLA Modules:
  0.0 198.4 jit_solution(6470733525801550442)
XLA Ops:
  0.7 1.3 reduce_sum.74
  2.0 0.9 convolution_bitcast_fusion.5
  4.3 11.7 %all-to-all-start.2 = ((f32[64,1,65]{2,1,0:T(1,128)}), f32[64,1,65]{2,1,0:T(1,128)S(1)}, u32[]{:S(2)}, u32[]{:S(2)}) async-start(f32[64,1,65]{2,1,0:T(1,128)} %broadcast_in_dim.26), calls=%async_computation.2 | async-start | bytes 65536 | tf_op jit(solution)/shard_map/while/body/eval_jaxpr/all_to_all | solution.py:14
  16.1 9.3 %all-to-all-done.2 = f32[64,1,65]{2,1,0:T(1,128)S(1)} async-done(((f32[64,1,65]{2,1,0:T(1,128)}), f32[64,1,65]{2,1,0:T(1,128)S(1)}, u32[]{:S(2)}, u32[]{:S(2)}) %all-to-all-start.2) | async-done | bytes 16672 | tf_op jit(solution)/shard_map/while/body/eval_jaxpr/all_to_all | solution.py:14
  27.4 72.4 %while.35 = (s32[]{:T(128)}, f32[128]{0:T(128)S(1)}, f32[64]{0:T(128)S(1)}, f32[4,128]{1,0:T(4,128)S(1)}, f32[128]{0:T(128)S(1)}, /*index=5*/f32[64,128]{1,0:T(8...) while((s32[]{:T(128)}, f32[128]{0:T(128)S(1)}, f32[64]{0:T(128)S(1)}, ...), condition=%wide.region_5.6_spmd, body=%wide.region_2.5_spmd.sunk | while | flops 201538 | bytes 186813 | solution.py:56
  28.3 0.8 pad_maximum_fusion.6
  29.7 5.0 %all-to-all-start = ((f32[64,1,65]{2,1,0:T(1,128)}), f32[64,1,65]{2,1,0:T(1,128)S(1)}, u32[]{:S(2)}, u32[]{:S(2)}) async-start(f32[64,1,65]{2,1,0:T(1,128)} %broadcast_in_dim.31), calls=%async_computation | async-start | bytes 65536 | tf_op jit(solution)/shard_map/while/body/eval_jaxpr/while/body/eval_jaxpr/all_to_all | solution.py:14
  34.7 9.5 %all-to-all-done = f32[64,1,65]{2,1,0:T(1,128)S(1)} async-done(((f32[64,1,65]{2,1,0:T(1,128)}), f32[64,1,65]{2,1,0:T(1,128)S(1)}, u32[]{:S(2)}, u32[]{:S(2)}) %all-to-all-start) | async-done | bytes 16672 | tf_op jit(solution)/shard_map/while/body/eval_jaxpr/while/body/eval_jaxpr/all_to_all | solution.py:14
  47.8 5.0 %all-to-all-start = ((f32[64,1,65]{2,1,0:T(1,128)}), f32[64,1,65]{2,1,0:T(1,128)S(1)}, u32[]{:S(2)}, u32[]{:S(2)}) async-start(f32[64,1,65]{2,1,0:T(1,128)} %broadcast_in_dim.31), calls=%async_computation | async-start | bytes 65536 | tf_op jit(solution)/shard_map/while/body/eval_jaxpr/while/body/eval_jaxpr/all_to_all | solution.py:14
  52.8 9.5 %all-to-all-done = f32[64,1,65]{2,1,0:T(1,128)S(1)} async-done(((f32[64,1,65]{2,1,0:T(1,128)}), f32[64,1,65]{2,1,0:T(1,128)S(1)}, u32[]{:S(2)}, u32[]{:S(2)}) %all-to-all-start) | async-done | bytes 16672 | tf_op jit(solution)/shard_map/while/body/eval_jaxpr/while/body/eval_jaxpr/all_to_all | solution.py:14
  65.9 5.0 %all-to-all-start = ((f32[64,1,65]{2,1,0:T(1,128)}), f32[64,1,65]{2,1,0:T(1,128)S(1)}, u32[]{:S(2)}, u32[]{:S(2)}) async-start(f32[64,1,65]{2,1,0:T(1,128)} %broadcast_in_dim.31), calls=%async_computation | async-start | bytes 65536 | tf_op jit(solution)/shard_map/while/body/eval_jaxpr/while/body/eval_jaxpr/all_to_all | solution.py:14
  70.9 9.5 %all-to-all-done = f32[64,1,65]{2,1,0:T(1,128)S(1)} async-done(((f32[64,1,65]{2,1,0:T(1,128)}), f32[64,1,65]{2,1,0:T(1,128)S(1)}, u32[]{:S(2)}, u32[]{:S(2)}) %all-to-all-start) | async-done | bytes 16672 | tf_op jit(solution)/shard_map/while/body/eval_jaxpr/while/body/eval_jaxpr/all_to_all | solution.py:14
  84.0 5.0 %all-to-all-start = ((f32[64,1,65]{2,1,0:T(1,128)}), f32[64,1,65]{2,1,0:T(1,128)S(1)}, u32[]{:S(2)}, u32[]{:S(2)}) async-start(f32[64,1,65]{2,1,0:T(1,128)} %broadcast_in_dim.31), calls=%async_computation | async-start | bytes 65536 | tf_op jit(solution)/shard_map/while/body/eval_jaxpr/while/body/eval_jaxpr/all_to_all | solution.py:14
  89.1 9.5 %all-to-all-done = f32[64,1,65]{2,1,0:T(1,128)S(1)} async-done(((f32[64,1,65]{2,1,0:T(1,128)}), f32[64,1,65]{2,1,0:T(1,128)S(1)}, u32[]{:S(2)}, u32[]{:S(2)}) %all-to-all-start) | async-done | bytes 16672 | tf_op jit(solution)/shard_map/while/body/eval_jaxpr/while/body/eval_jaxpr/all_to_all | solution.py:14
  99.9 1.3 collective-permute-start
  101.2 0.8 collective-permute-done
  102.7 0.8 pad_maximum_fusion.3
  104.1 5.0 %all-to-all-start.3 = ((f32[64,1,65]{2,1,0:T(1,128)}), f32[64,1,65]{2,1,0:T(1,128)S(1)}, u32[]{:S(2)}, u32[]{:S(2)}) async-start(f32[64,1,65]{2,1,0:T(1,128)} %broadcast_in_dim.27), calls=%async_computation.3 | async-start | bytes 65536 | tf_op jit(solution)/shard_map/all_to_all | solution.py:14
  109.1 9.5 %all-to-all-done.3 = f32[64,1,65]{2,1,0:T(1,128)S(1)} async-done(((f32[64,1,65]{2,1,0:T(1,128)}), f32[64,1,65]{2,1,0:T(1,128)S(1)}, u32[]{:S(2)}, u32[]{:S(2)}) %all-to-all-start.3) | async-done | bytes 16672 | tf_op jit(solution)/shard_map/all_to_all | solution.py:14
  120.1 77.8 %while.36 = (s32[]{:T(128)}, f32[128]{0:T(128)S(1)}, f32[64]{0:T(128)S(1)}, f32[4,128]{1,0:T(4,128)}, f32[4]{0:T(128)S(1)}, /*index=5*/f32[4,128]{1,0:T(4,128)S(...) while((s32[]{:T(128)}, f32[128]{0:T(128)S(1)}, ...), condition=%wide.region_11.12_spmd, body=%wide.region_8.0_spmd.sunk | while | flops 201666 | bytes 188921 | solution.py:56
  122.4 5.0 %all-to-all-start.1 = ((f32[64,1,65]{2,1,0:T(1,128)}), f32[64,1,65]{2,1,0:T(1,128)S(1)}, u32[]{:S(2)}, u32[]{:S(2)}) async-start(f32[64,1,65]{2,1,0:T(1,128)} %broadcast_in_dim.32), calls=%async_computation.1 | async-start | bytes 65536 | tf_op jit(solution)/shard_map/while/body/eval_jaxpr/all_to_all | solution.py:14
  127.4 9.5 %all-to-all-done.1 = f32[64,1,65]{2,1,0:T(1,128)S(1)} async-done(((f32[64,1,65]{2,1,0:T(1,128)}), f32[64,1,65]{2,1,0:T(1,128)S(1)}, u32[]{:S(2)}, u32[]{:S(2)}) %all-to-all-start.1) | async-done | bytes 16672 | tf_op jit(solution)/shard_map/while/body/eval_jaxpr/all_to_all | solution.py:14
  138.3 1.3 dynamic_update_slice.10
  141.8 5.0 %all-to-all-start.1 = ((f32[64,1,65]{2,1,0:T(1,128)}), f32[64,1,65]{2,1,0:T(1,128)S(1)}, u32[]{:S(2)}, u32[]{:S(2)}) async-start(f32[64,1,65]{2,1,0:T(1,128)} %broadcast_in_dim.32), calls=%async_computation.1 | async-start | bytes 65536 | tf_op jit(solution)/shard_map/while/body/eval_jaxpr/all_to_all | solution.py:14
  146.8 9.5 %all-to-all-done.1 = f32[64,1,65]{2,1,0:T(1,128)S(1)} async-done(((f32[64,1,65]{2,1,0:T(1,128)}), f32[64,1,65]{2,1,0:T(1,128)S(1)}, u32[]{:S(2)}, u32[]{:S(2)}) %all-to-all-start.1) | async-done | bytes 16672 | tf_op jit(solution)/shard_map/while/body/eval_jaxpr/all_to_all | solution.py:14
  157.8 1.3 dynamic_update_slice.10
  161.3 5.0 %all-to-all-start.1 = ((f32[64,1,65]{2,1,0:T(1,128)}), f32[64,1,65]{2,1,0:T(1,128)S(1)}, u32[]{:S(2)}, u32[]{:S(2)}) async-start(f32[64,1,65]{2,1,0:T(1,128)} %broadcast_in_dim.32), calls=%async_computation.1 | async-start | bytes 65536 | tf_op jit(solution)/shard_map/while/body/eval_jaxpr/all_to_all | solution.py:14
  166.3 9.5 %all-to-all-done.1 = f32[64,1,65]{2,1,0:T(1,128)S(1)} async-done(((f32[64,1,65]{2,1,0:T(1,128)}), f32[64,1,65]{2,1,0:T(1,128)S(1)}, u32[]{:S(2)}, u32[]{:S(2)}) %all-to-all-start.1) | async-done | bytes 16672 | tf_op jit(solution)/shard_map/while/body/eval_jaxpr/all_to_all | solution.py:14
  177.2 1.3 dynamic_update_slice.10
  180.7 5.0 %all-to-all-start.1 = ((f32[64,1,65]{2,1,0:T(1,128)}), f32[64,1,65]{2,1,0:T(1,128)S(1)}, u32[]{:S(2)}, u32[]{:S(2)}) async-start(f32[64,1,65]{2,1,0:T(1,128)} %broadcast_in_dim.32), calls=%async_computation.1 | async-start | bytes 65536 | tf_op jit(solution)/shard_map/while/body/eval_jaxpr/all_to_all | solution.py:14
  185.7 9.5 %all-to-all-done.1 = f32[64,1,65]{2,1,0:T(1,128)S(1)} async-done(((f32[64,1,65]{2,1,0:T(1,128)}), f32[64,1,65]{2,1,0:T(1,128)S(1)}, u32[]{:S(2)}, u32[]{:S(2)}) %all-to-all-start.1) | async-done | bytes 16672 | tf_op jit(solution)/shard_map/while/body/eval_jaxpr/all_to_all | solution.py:14
  196.7 1.3 dynamic_update_slice.10
  (101 shorter events, 28.1 us)
Async XLA Ops:
  0.6 15.3 %copy-start = (f32[128,256]{1,0:T(8,128)S(1)}, f32[128,256]{1,0:T(8,128)}, u32[]{:S(2)}) copy-start(f32[128,256]{1,0:T(8,128)} %param.11) | copy-start | bytes 393220
  0.6 1.3 copy-start.4
  4.3 11.7 %copy-start.5 = (s32[4]{0:T(128)S(1)}, s32[4]{0:T(128)}, u32[]{:S(2)}) copy-start(s32[4]{0:T(128)} %param.10) | copy-start | bytes 52
  4.3 21.2 %all-to-all-start.2 = ((f32[64,1,65]{2,1,0:T(1,128)}), f32[64,1,65]{2,1,0:T(1,128)S(1)}, u32[]{:S(2)}, u32[]{:S(2)}) async-start(f32[64,1,65]{2,1,0:T(1,128)} %broadcast_in_dim.26), calls=%async_computation.2 | async-start | bytes 65536 | tf_op jit(solution)/shard_map/while/body/eval_jaxpr/all_to_all | solution.py:14
  15.9 10.9 %copy-start.2 = (f32[1,64,128]{2,1,0:T(8,128)S(1)}, f32[1,64,128]{2,1,0:T(8,128)}, u32[]{:S(2)}) copy-start(f32[1,64,128]{2,1,0:T(8,128)} %param.14) | copy-start | bytes 98308
  16.1 10.7 %copy-start.1 = (f32[1,64,128]{2,1,0:T(8,128)S(1)}, f32[1,64,128]{2,1,0:T(8,128)}, u32[]{:S(2)}) copy-start(f32[1,64,128]{2,1,0:T(8,128)} %param.13) | copy-start | bytes 98308
  26.8 0.7 copy-start.3
  29.7 14.5 %all-to-all-start = ((f32[64,1,65]{2,1,0:T(1,128)}), f32[64,1,65]{2,1,0:T(1,128)S(1)}, u32[]{:S(2)}, u32[]{:S(2)}) async-start(f32[64,1,65]{2,1,0:T(1,128)} %broadcast_in_dim.31), calls=%async_computation | async-start | bytes 65536 | tf_op jit(solution)/shard_map/while/body/eval_jaxpr/while/body/eval_jaxpr/all_to_all | solution.py:14
  47.8 14.5 %all-to-all-start = ((f32[64,1,65]{2,1,0:T(1,128)}), f32[64,1,65]{2,1,0:T(1,128)S(1)}, u32[]{:S(2)}, u32[]{:S(2)}) async-start(f32[64,1,65]{2,1,0:T(1,128)} %broadcast_in_dim.31), calls=%async_computation | async-start | bytes 65536 | tf_op jit(solution)/shard_map/while/body/eval_jaxpr/while/body/eval_jaxpr/all_to_all | solution.py:14
  65.9 14.5 %all-to-all-start = ((f32[64,1,65]{2,1,0:T(1,128)}), f32[64,1,65]{2,1,0:T(1,128)S(1)}, u32[]{:S(2)}, u32[]{:S(2)}) async-start(f32[64,1,65]{2,1,0:T(1,128)} %broadcast_in_dim.31), calls=%async_computation | async-start | bytes 65536 | tf_op jit(solution)/shard_map/while/body/eval_jaxpr/while/body/eval_jaxpr/all_to_all | solution.py:14
  84.0 14.5 %all-to-all-start = ((f32[64,1,65]{2,1,0:T(1,128)}), f32[64,1,65]{2,1,0:T(1,128)S(1)}, u32[]{:S(2)}, u32[]{:S(2)}) async-start(f32[64,1,65]{2,1,0:T(1,128)} %broadcast_in_dim.31), calls=%async_computation | async-start | bytes 65536 | tf_op jit(solution)/shard_map/while/body/eval_jaxpr/while/body/eval_jaxpr/all_to_all | solution.py:14
  99.9 2.1 %collective-permute-start = (f32[128]{0:T(128)S(1)}, f32[128]{0:T(128)S(1)}, u32[]{:S(2)}, u32[]{:S(2)}) collective-permute-start(f32[128]{0:T(128)S(1)} %get-tuple-element.111), channel_id=1, source_target_pairs={{0,1},{2,3},{4,5},{6,7},{8,9},{10,11},{12,13},{14,15},{16,17},{18,... | collective-permute-start | bytes 1544 | tf_op jit(solution)/shard_map/while/body/eval_jaxpr/ppermute | solution.py:32
  104.1 14.5 %all-to-all-start.3 = ((f32[64,1,65]{2,1,0:T(1,128)}), f32[64,1,65]{2,1,0:T(1,128)S(1)}, u32[]{:S(2)}, u32[]{:S(2)}) async-start(f32[64,1,65]{2,1,0:T(1,128)} %broadcast_in_dim.27), calls=%async_computation.3 | async-start | bytes 65536 | tf_op jit(solution)/shard_map/all_to_all | solution.py:14
  122.4 14.5 %all-to-all-start.1 = ((f32[64,1,65]{2,1,0:T(1,128)}), f32[64,1,65]{2,1,0:T(1,128)S(1)}, u32[]{:S(2)}, u32[]{:S(2)}) async-start(f32[64,1,65]{2,1,0:T(1,128)} %broadcast_in_dim.32), calls=%async_computation.1 | async-start | bytes 65536 | tf_op jit(solution)/shard_map/while/body/eval_jaxpr/all_to_all | solution.py:14
  141.8 14.5 %all-to-all-start.1 = ((f32[64,1,65]{2,1,0:T(1,128)}), f32[64,1,65]{2,1,0:T(1,128)S(1)}, u32[]{:S(2)}, u32[]{:S(2)}) async-start(f32[64,1,65]{2,1,0:T(1,128)} %broadcast_in_dim.32), calls=%async_computation.1 | async-start | bytes 65536 | tf_op jit(solution)/shard_map/while/body/eval_jaxpr/all_to_all | solution.py:14
  161.3 14.5 %all-to-all-start.1 = ((f32[64,1,65]{2,1,0:T(1,128)}), f32[64,1,65]{2,1,0:T(1,128)S(1)}, u32[]{:S(2)}, u32[]{:S(2)}) async-start(f32[64,1,65]{2,1,0:T(1,128)} %broadcast_in_dim.32), calls=%async_computation.1 | async-start | bytes 65536 | tf_op jit(solution)/shard_map/while/body/eval_jaxpr/all_to_all | solution.py:14
  180.7 14.5 %all-to-all-start.1 = ((f32[64,1,65]{2,1,0:T(1,128)}), f32[64,1,65]{2,1,0:T(1,128)S(1)}, u32[]{:S(2)}, u32[]{:S(2)}) async-start(f32[64,1,65]{2,1,0:T(1,128)} %broadcast_in_dim.32), calls=%async_computation.1 | async-start | bytes 65536 | tf_op jit(solution)/shard_map/while/body/eval_jaxpr/all_to_all | solution.py:14
  197.9 0.5 copy-start.6
where the time goes:
time: 199 us; the launch traced here: 198 us
  waiting for transfers between devices  96 us (48%)
  starting transfers between devices  58 us (29%)
  local copies, waits for them, and re-layouts  18.8 us (9%)
  other arithmetic  9.86 us (5%)
  matrix products  8.24 us (4%)
  loops' own time  5.35 us (3%)
  between operations  2.21 us (1%)
    all_to_all x10, waiting for transfers between devices, copy_for_each(): return lax.all_to_all(copies, axis, split_axis=0, concat_axis=0, tiled=True)  95.2 us
    all_to_all x10, starting transfers between devices, copy_for_each(): return lax.all_to_all(copies, axis, split_axis=0, concat_axis=0, tiled=True)  56.7 us
    concatenate x10, other arithmetic, in_one(): running = over_copies(jnp.concatenate([a.ravel() for a in arrays]), axis)  7.52 us
    broadcast_in_dim x10, local copies, waits for them, and re-layouts, copy_for_each(): copies = jnp.broadcast_to(array, (lax.axis_size(axis), *array.shape))  6.21 us
    dot_general x8, matrix products, frame(): jnp.dot(mixture_now, right_rows, precision=PRECISE)  5.96 us
    slice x10, local copies, waits for them, and re-layouts, in_one(): running[b:e].reshape(a.shape)  5.89 us
    dynamic_update_slice x8, local copies, waits for them, and re-layouts, run_span(): lax.scan(frame, (belief, mixture), emitted_all)  5.56 us
    another operation x2, loops' own time, run_span(): lax.scan(frame, (belief, mixture), emitted_all)  5.35 us
  transfers between devices with their start and end apart: 11, of which 11 were waited for; matrix products, arithmetic and copies ran while one was open for 0% of the time, Pallas kernels for 0%

commit v1 on v0

v1 whole, which is shorter than its diff:
```python
import functools

import jax
import jax.numpy as jnp
from jax import lax
from jax.experimental import pallas as pl
from jax.experimental.pallas import tpu as pltpu
from jax.sharding import PartitionSpec as P

MESH = pl.DeviceIdType.MESH
PRECISE = lax.Precision.HIGHEST
LANES = 128
R = 64
F = 4
ROWS = 8 * R


def nt(a, b):
    return lax.dot_general(
        a, b, (((1,), (1,)), ((), ())), precision=PRECISE, preferred_element_type=jnp.float32
    )


def nn(a, b):
    return jnp.dot(a, b, precision=PRECISE, preferred_element_type=jnp.float32)


def iota(shape, axis):
    return lax.broadcasted_iota(jnp.int32, shape, axis)


def chain(e, d):
    p = [jnp.ones_like(d)]
    for r in range(F):
        p.append(p[-1] * (e[r : r + 1] * d))
    return p, [1.0 / (p[s] * d) for s in range(F)]


def kernel(
    dims,
    states,
    sym_hbm,
    emis_hbm,
    decay_hbm,
    left_hbm,
    right_hbm,
    init_hbm,
    out_ref,
    log_ref,
    sym,
    emis,
    dec,
    uv,
    init,
    other,
    emit,
    emit_other,
    part,
    rs_buf,
    line_src,
    line_buf,
    whole_src,
    whole,
    in_sem,
    send_sem,
    recv_sem,
):
    nz, ny, nx = dims
    plane = ny * nx
    piece = ROWS // plane
    tm = lax.axis_index("tm")
    core = lax.axis_index("state")
    x = lax.rem(tm, nx)
    y = lax.rem(lax.div(tm, nx), ny)
    z = lax.div(tm, plane)
    mine = y * nx + x

    def plane_peer(k):
        yy = lax.rem(y + k // nx, ny)
        xx = lax.rem(x + k % nx, nx)
        place = yy * nx + xx
        return place, z * plane + place

    def line_peer(k):
        return lax.rem(z + k, nz) * plane + mine

    barrier = pltpu.get_barrier_semaphore()

    def hail(target, on):
        pl.semaphore_signal(barrier, inc=1, device_id=(target, on), device_id_type=MESH)

    loads = [
        pltpu.make_async_copy(sym_hbm, sym, in_sem.at[0]),
        pltpu.make_async_copy(emis_hbm, emis, in_sem.at[1]),
        pltpu.make_async_copy(decay_hbm, dec, in_sem.at[2]),
        pltpu.make_async_copy(left_hbm.at[0], uv.at[0], in_sem.at[3]),
        pltpu.make_async_copy(right_hbm.at[0], uv.at[1], in_sem.at[4]),
        pltpu.make_async_copy(init_hbm, init, in_sem.at[5]),
    ]
    for load in loads:
        load.start()
    hail(tm, 1 - core)
    for k in range(1, plane):
        for on in range(2):
            hail(plane_peer(k)[1], on)
    for k in range(1, nz):
        hail(line_peer(k), core)
    for load in loads:
        load.wait()

    rows8 = iota((8, 256), 0)
    wanted = jnp.full((8, 256), -1, jnp.int32)
    for r in range(F):
        wanted = jnp.where(rows8 == r, sym[r], wanted)
    onehot = jnp.where(iota((8, 256), 1) == wanted, 1.0, 0.0)
    emitted = nt(onehot, emis[...])
    emit[...] = jnp.where(iota((8, LANES), 0) == F, dec[...], emitted)
    pl.semaphore_wait(barrier, 2 * (plane - 1) + nz)

    swaps = [
        pltpu.make_async_remote_copy(
            src_ref=uv.at[1 - core],
            dst_ref=other,
            send_sem=send_sem.at[0],
            recv_sem=recv_sem.at[0],
            device_id=(tm, 1 - core),
            device_id_type=MESH,
        ),
        pltpu.make_async_remote_copy(
            src_ref=emit,
            dst_ref=emit_other,
            send_sem=send_sem.at[1],
            recv_sem=recv_sem.at[1],
            device_id=(tm, 1 - core),
            device_id_type=MESH,
        ),
    ]
    for swap in swaps:
        swap.start()
    for swap in swaps:
        swap.wait()

    first = core == 0
    u_own = uv[0] * (1.0 / states)
    v_own = uv[1]
    u_hi = jnp.where(first, other[...], uv[0]) * (1.0 / states)
    v_lo = jnp.where(first, uv[1], other[...])
    e_own = emit[...]
    e_lo = jnp.where(first, emit[...], emit_other[...])
    e_hi = jnp.where(first, emit_other[...], emit[...])
    p_own, w_own = chain(e_own, e_own[F : F + 1])
    p_lo, w_lo = chain(e_lo, e_lo[F : F + 1])
    p_hi, w_hi = chain(e_hi, e_hi[F : F + 1])
    p_all = p_lo + [p_lo[F] * p_hi[r] for r in range(1, F + 1)]
    beta0 = init[...].reshape(1, LANES)

    zero = jnp.zeros((1, LANES), jnp.float32)
    tail = [jnp.where(first, p_all[t], zero) for t in range(F + 1, 2 * F + 1)]
    p_rows = jnp.concatenate(p_own[1:] + tail, axis=0)
    t_of_row = iota((8, LANES), 0) + 1
    quota = [
        jnp.where(t_of_row > s, p_rows * (e_own[F : F + 1] * w_own[s]), 0.0) for s in range(F)
    ]
    right0 = jnp.concatenate(quota + [jnp.zeros((R - 8 * F, LANES), jnp.float32), u_own * p_own[1]])
    part[0:R, :] = nt(v_own * w_own[0], right0)
    right1 = jnp.concatenate([u_own * p_own[2], u_own * p_own[3]])
    part[R : 4 * R, :] = nt(jnp.concatenate([v_own * w_own[s] for s in range(3)]), right1)
    p_a = p_all[F] * jnp.where(first, p_hi[0], p_hi[2])
    p_b = p_all[F] * jnp.where(first, p_hi[1], p_hi[3])
    right2 = jnp.concatenate([u_hi * p_a, u_hi * p_b])
    part[4 * R :, :] = nt(jnp.concatenate([v_lo * w_lo[s] for s in range(F)]), right2)

    starts = jnp.concatenate([p * beta0 for p in p_all] + [jnp.zeros((7, LANES), jnp.float32)])
    led = nt(starts[:8], jnp.concatenate([u_own, u_hi]))
    led = jnp.where(iota((8, LANES), 0) < F, led, pltpu.roll(led, R, 1))
    sums = jnp.broadcast_to(jnp.sum(starts, axis=1, keepdims=True), (16, LANES))
    low = iota((8, LANES), 1) < R
    part[3 * R : 3 * R + 8, :] = jnp.where(low, led, part[3 * R : 3 * R + 8, :])
    low16 = iota((16, LANES), 1) < R
    part[3 * R + 16 : 3 * R + 32, :] = jnp.where(low16, sums, part[3 * R + 16 : 3 * R + 32, :])

    def at_piece(p):
        return pl.ds(pl.multiple_of(p * piece, piece), piece)

    for k in range(1, plane):
        place, chip = plane_peer(k)
        pltpu.make_async_remote_copy(
            src_ref=part.at[at_piece(place)],
            dst_ref=rs_buf.at[k - 1],
            send_sem=send_sem.at[2],
            recv_sem=recv_sem.at[2],
            device_id=(chip, core),
            device_id_type=MESH,
        ).start()
    drain = pltpu.make_async_remote_copy(
        src_ref=rs_buf,
        dst_ref=rs_buf,
        send_sem=send_sem.at[2],
        recv_sem=recv_sem.at[2],
        device_id=(tm, 1 - core),
        device_id_type=MESH,
    )
    drain.wait_recv()
    total = part[at_piece(mine), :]
    for k in range(plane - 1):
        total = total + rs_buf[k]
    line_src[...] = total

    for k in range(1, nz):
        pltpu.make_async_remote_copy(
            src_ref=line_src,
            dst_ref=line_buf.at[k - 1],
            send_sem=send_sem.at[3],
            recv_sem=recv_sem.at[3],
            device_id=(line_peer(k), core),
            device_id_type=MESH,
        ).start()
    line_drain = pltpu.make_async_remote_copy(
        src_ref=line_buf,
        dst_ref=line_buf,
        send_sem=send_sem.at[3],
        recv_sem=recv_sem.at[3],
        device_id=(tm, 1 - core),
        device_id_type=MESH,
    )
    line_drain.wait_recv()
    for k in range(nz - 1):
        total = total + line_buf[k]
    whole_src[...] = total
    here = pl.ds(pl.multiple_of(core * ROWS + mine * piece, piece), piece)
    whole[here, :] = total

    def give(chip, on):
        pltpu.make_async_remote_copy(
            src_ref=whole_src,
            dst_ref=whole.at[here],
            send_sem=send_sem.at[4],
            recv_sem=recv_sem.at[4],
            device_id=(chip, on),
            device_id_type=MESH,
        ).start()

    for k in range(1, plane):
        give(plane_peer(k)[1], 1)
    early = jnp.logical_and(first, mine < plane // 2)

    @pl.when(first)
    def _():
        give(tm, 1)

    @pl.when(early)
    def _():
        for k in range(1, plane):
            give(plane_peer(k)[1], 0)

    def taken(rows):
        return pltpu.make_async_remote_copy(
            src_ref=whole.at[pl.ds(0, rows)],
            dst_ref=whole.at[pl.ds(0, rows)],
            send_sem=send_sem.at[4],
            recv_sem=recv_sem.at[4],
            device_id=(tm, 1 - core),
            device_id_type=MESH,
        )

    @pl.when(jnp.logical_not(first))
    def _():
        taken((2 * plane - 1) * piece).wait_recv()

    @pl.when(early)
    def _():
        taken((plane // 2 - 1) * piece).wait_recv()

    @pl.when(jnp.logical_and(first, mine >= plane // 2))
    def _():
        taken((plane // 2) * piece).wait_recv()

    lane8 = iota((8, LANES), 1)
    row8 = iota((8, LANES), 0)
    high = lane8 >= R

    def pair(base, q):
        a0 = whole[base + 2 * q : base + 2 * q + 1, :]
        a1 = whole[base + 2 * q + 1 : base + 2 * q + 2, :]
        a0 = jnp.broadcast_to(a0, (8, LANES))
        a1 = pltpu.roll(jnp.broadcast_to(a1, (8, LANES)), R, 1)
        return jnp.where(high, a1, a0)

    def close(a, top):
        return a + jnp.where(high, nn(a[:, :R], whole[top : top + R, :]), 0.0)

    def spread(xs, at):
        rows = jnp.zeros((8, LANES), jnp.float32)
        for q, xq in enumerate(xs):
            for h in range(2):
                keep = jnp.logical_and(row8 == at + 2 * q + h, high == (h == 1))
                rows = jnp.where(keep, xq, rows)
        return rows

    def twice(a):
        return jnp.concatenate([a, a], axis=0)

    E_AT = 3 * R
    x0 = close(pair(E_AT, 0), 0)
    x1 = close(pair(E_AT, 1) + nn(x0, whole[R : 3 * R, :]), 3 * R)
    rows_lo = spread([x0, x1], 0)
    y_lo = nn(rows_lo, twice(v_lo))
    tally_lo = nn(rows_lo, twice(whole[0:R, :]))

    def start_sum(t):
        return whole[E_AT + 16 + t : E_AT + 17 + t, 0:1]

    def tally(table, t):
        keep = jnp.logical_and(lane8 == 8 * row8 + (t - 1), row8 < F)
        return jnp.sum(jnp.where(keep, table, 0.0), keepdims=True)

    def finish(gamma, y, w, p, sums):
        for r in range(F):
            gamma = gamma + w[r] * y[r : r + 1]
            out_ref[r : r + 1, :] = p[r] * gamma * (states / sums[r + 1])
            log_ref[r : r + 1, :] = jnp.broadcast_to(jnp.log(sums[r + 1] / sums[r]), (1, LANES))
        log_ref[F:8, :] = jnp.zeros((8 - F, LANES), jnp.float32)

    @pl.when(first)
    def _():
        sums = [start_sum(0)] + [start_sum(t) + tally(tally_lo, t) for t in range(1, F + 1)]
        finish(beta0, y_lo, w_lo, p_all[1 : F + 1], sums)

    @pl.when(jnp.logical_not(first))
    def _():
        c0, c1 = (ROWS + k * R for k in (0, 3))
        x2 = pair(E_AT, 2) + nn(x0, whole[4 * R : 6 * R, :]) + nn(x1, whole[6 * R : 8 * R, :])
        x2 = close(x2, c0)
        x3 = pair(E_AT, 3) + nn(x0, whole[ROWS + 4 * R : ROWS + 6 * R, :])
        x3 = x3 + nn(x1, whole[ROWS + 6 * R : ROWS + 8 * R, :])
        x3 = close(x3 + nn(x2, whole[ROWS + R : ROWS + 3 * R, :]), c1)
        rows_hi = spread([x2, x3], 0)
        y_hi = nn(rows_hi, twice(v_own))
        tally_hi = nn(rows_hi, twice(whole[c0 : c0 + R, :]))
        sums = [start_sum(F) + tally(tally_lo, F)]
        for t in range(1, F + 1):
            sums.append(start_sum(F + t) + tally(tally_lo, F + t) + tally(tally_hi, t))
        gamma = beta0
        for r in range(F):
            gamma = gamma + w_lo[r] * y_lo[r : r + 1]
        w = [w_hi[r] / p_lo[F] for r in range(F)]
        finish(gamma, y_hi, w, p_all[F + 1 :], sums)

    drain.wait_send()
    line_drain.wait_send()
    taken((plane - 1) * piece).wait_send()

    @pl.when(first)
    def _():
        taken(piece).wait_send()

    @pl.when(early)
    def _():
        taken((plane - 1) * piece).wait_send()


def solution(mesh, dims=(4, 4, 4)):
    states = LANES * mesh.shape["tm"]
    plane = dims[1] * dims[2]
    piece = ROWS // plane

    def per_device(symbols, emission, decay, left_factor, right_factor, initial):
        f32 = jnp.float32
        filtered, logs = pl.pallas_call(
            functools.partial(kernel, dims, states),
            out_shape=(
                jax.ShapeDtypeStruct((F, LANES), f32),
                jax.ShapeDtypeStruct((8, LANES), f32),
            ),
            in_specs=[pl.BlockSpec(memory_space=pl.ANY)] * 6,
            out_specs=(pl.BlockSpec(memory_space=pltpu.VMEM),) * 2,
            scratch_shapes=[
                pltpu.SMEM((F,), jnp.int32),
                pltpu.VMEM((LANES, 256), f32),
                pltpu.VMEM((1, LANES), f32),
                pltpu.VMEM((2, R, LANES), f32),
                pltpu.VMEM((LANES,), f32),
                pltpu.VMEM((R, LANES), f32),
                pltpu.VMEM((8, LANES), f32),
                pltpu.VMEM((8, LANES), f32),
                pltpu.VMEM((ROWS, LANES), f32),
                pltpu.VMEM((plane - 1, piece, LANES), f32),
                pltpu.VMEM((piece, LANES), f32),
                pltpu.VMEM((dims[0] - 1, piece, LANES), f32),
                pltpu.VMEM((piece, LANES), f32),
                pltpu.VMEM((2 * ROWS, LANES), f32),
                pltpu.SemaphoreType.DMA((6,)),
                pltpu.SemaphoreType.DMA((5,)),
                pltpu.SemaphoreType.DMA((5,)),
            ],
            compiler_params=pltpu.CompilerParams(collective_id=0, has_side_effects=True),
        )(symbols, emission, decay, left_factor, right_factor, initial)
        return filtered, logs[:F, 0]

    return jax.shard_map(
        per_device,
        mesh=mesh,
        in_specs=(
            P("state"),
            P("tm", None),
            P("state", "tm"),
            P("state", None, "tm"),
            P("state", None, "tm"),
            P("tm"),
        ),
        out_specs=(P("state", "tm"), P("state")),
        check_vma=False,
    )
```

time: 199 us -> 31.8 us (0.16)
  the two profiles are of different devices: /device:TPU:0 before, /device:TPU:1 now
where the time goes in v1:
time: 31.8 us; the launch traced here: 31.7 us
  Pallas kernels  29.2 us (92%)
  local copies, waits for them, and re-layouts  1.89 us (6%)
  between operations  0.65 us (2%)
    pallas_call x1, Pallas kernels, per_device(): pl.pallas_call(functools.partial(kernel, dims, states), out_shape=(jax.Sh...  29.2 us
    slice x1, local copies, waits for them, and re-layouts, per_device(): return (filtered, logs[:F, 0])  1.31 us

profile of v1, /device:TPU:1, one launch (start us, length us, event | category | flops | bytes accessed | tf_op | source)
XLA Modules:
  0.0 31.7 jit_solution(15010940045479749035)
XLA Ops:
  0.6 29.2 %shard_map.77 = (f32[4,128]{1,0:T(4,128)}, f32[8,128]{1,0:T(8,128)}) custom-call(s32[4]{0:T(128)} %sym_hbm.1, f32[128,256]{1,0:T(8,128)} %emis_hbm.1, f32[1,128]{1,0:T(1,128)} %decay_hbm.1, f32[1,64,128]{2,1,0:T(8,128)} %left_hbm.1, f32[1,64,128]{2,1,0:T(8,128)} %right_hbm.1, f32[128]{0:T(128)} %init_hbm.1), custom_call_target="tpu_custom_call" | custom-call | tf_op jit(solution)/shard_map/pallas_call | solution.py:369
  29.8 0.0 copy-start
  29.8 1.3 %slice_reduce_fusion = f32[4]{0:T(128)} fusion(f32[8,128]{1,0:T(8,128)} %get-tuple-element.5), kind=kLoop, calls=%fused_computation | loop fusion | bytes 32 | tf_op jit(solution)/shard_map/slice | solution.py:398
  31.1 0.0 copy-done
  31.1 0.6 %copy.9 = f32[4,128]{1,0:T(4,128)} copy(f32[4,128]{1,0:T(4,128)S(1)} %copy-done) | data formatting | bytes 4096
Async XLA Ops:
  29.8 1.3 %copy-start = (f32[4,128]{1,0:T(4,128)S(1)}, f32[4,128]{1,0:T(4,128)}, u32[]{:S(2)}) copy-start(f32[4,128]{1,0:T(4,128)} %get-tuple-element.8) | copy-start | bytes 6148
